TPU v7x, 32 devices: a whole 2x2x4 slice. The times are simulated.
32 devices in a mesh: pairs: 8 (over z, y), cols: 4 (over x, core).
Axes of the slice: x: 2, y: 2, z: 4, core: 2. Of those that a mesh axis runs over, the one named last changes fastest.
Arguments:
- amplitudes: bfloat16 [64, 256, 256], P('pairs', 'cols'), may hold values from -6 to 6
- pno_counts: int32 [64], P('pairs'), may hold values from 96 to 256
- fock_blocks: bfloat16 [64, 256, 256], P('pairs'), may hold values from -1 to 5, as said below
- exchange_blocks: bfloat16 [64, 256, 256], P('pairs', 'cols'), may hold values from -6 to 6
- intersections: bfloat16 [64, 32, 256, 256], P('pairs', None, 'cols'), may hold values from -0.375 to 0.375
- partners: int32 [64, 32], P('pairs'), may hold values from 0 to 63, as said below
- couplings: float32 [64, 32], P('pairs'), may hold values from -3 to 3
Outputs:
- residual_blocks: bfloat16 [64, 256, 256], P('pairs', 'cols')
Inputs may be any that keep to these rules, and one draw needn't show every extreme that they name: `partners`: within the coupling lists of one aligned block of 8 pairs, at most 64 entries name pairs of any one aligned block of 8 pairs, and exactly 64 do for some block. `fock_blocks`: each block is symmetric.
All inputs are finite; a program needn't handle non-finite values.
Results may differ from a plain program's by a relative error of at most 0.0022.
Values may be sent and summed in bfloat16 or wider, within the bound.
No kernel may reach another device: no remote copies, remote signals or barrier semaphores. Data moves between devices by JAX's collectives and lax.ppermute only.
A program may use at most 128 MiB of HBM per device.

v0:
```python
import jax
import jax.numpy as jnp
from jax import lax
from jax.sharding import PartitionSpec as P

CPL = 32


def shards(
    amplitudes, pno_counts, fock_blocks, exchange_blocks, intersections, partners, couplings
):
    local_pairs, share, width = amplitudes.shape
    column = lax.axis_index("cols")
    row_keep = column * share + jnp.arange(share, dtype=jnp.int32)[None, :] < pno_counts[:, None]
    col_keep = jnp.arange(width, dtype=jnp.int32)[None, :] < pno_counts[:, None]
    keep = row_keep[:, :, None] & col_keep[:, None, :]
    masked = jnp.where(keep, amplitudes, jnp.zeros_like(amplitudes))
    linear = partners.reshape(-1)
    empty = jnp.zeros((local_pairs * CPL, share, width), jnp.bfloat16)
    piece = lax.all_gather(masked, "pairs", axis=0, tiled=True)
    present = (linear >= 0) & (linear < piece.shape[0])
    picked = piece[jnp.clip(linear, 0, piece.shape[0] - 1)]
    partner_flat = jnp.where(present[:, None, None], picked, empty)
    partner_blocks = partner_flat.reshape(local_pairs, CPL, share, width)
    fock_cols = lax.dynamic_slice_in_dim(fock_blocks, column * share, share, 2)
    partial_value = jnp.einsum(
        "pab,pbc->pac", fock_cols, masked, preferred_element_type=jnp.float32
    )
    whole_intersections = lax.all_gather(intersections, "cols", axis=2, tiled=True)
    projected = jnp.einsum(
        "pqab,pqbc->pqac", partner_blocks, whole_intersections, preferred_element_type=jnp.float32
    ).astype(jnp.bfloat16)
    for slot_index in range(CPL):
        term = jnp.einsum(
            "pcd,pca->pda",
            intersections[:, slot_index],
            projected[:, slot_index],
            preferred_element_type=jnp.float32,
        )
        partial_value = partial_value + couplings[:, slot_index, None, None] * term
    summed = lax.psum_scatter(partial_value, "cols", scatter_dimension=1, tiled=True)
    fock_term = jnp.einsum("pab,pbc->pac", masked, fock_blocks, preferred_element_type=jnp.float32)
    total = exchange_blocks.astype(jnp.float32) + fock_term + summed
    return jnp.where(keep, total, jnp.zeros_like(total)).astype(jnp.bfloat16)


def solution(mesh):
    in_specs = (
        P("pairs", "cols", None),
        P("pairs"),
        P("pairs", None, None),
        P("pairs", "cols", None),
        P("pairs", None, "cols", None),
        P("pairs", None),
        P("pairs", None),
    )
    out_specs = P("pairs", "cols", None)
    return jax.shard_map(shards, mesh=mesh, in_specs=in_specs, out_specs=out_specs, check_vma=False)
```

profile of v0, /device:TPU:0, one launch (start us, length us, event | category | flops | bytes accessed | tf_op | source)
XLA Modules:
  0.0 406.6 jit_solution(1802354815083428256)
XLA Ops:
  8.1 1.8 and_select_fusion
  11.7 50.1 %all-gather.3.cloned.1.call-done = bf16[64,64,256]{2,1,0:T(8,128)(2,1)} async-done(((bf16[8,64,256]{2,1,0:T(8,128)(2,1)}), bf16[64,64,256]{2,1,0:T(8,128)(2,1)}) %all-gather.3.cloned.1.call-update) | async-done | bytes 2097168 | tf_op jit(solution)/shard_map/all_gather | solution.py:20
  61.9 12.4 %gather_fusion = bf16[256,64,256]{2,1,0:T(8,128)(2,1)} fusion(bf16[64,64,256]{2,1,0:T(8,128)(2,1)} %all-gather.3.cloned.1.call-done, s32[1024]{0:T(1024)S(1)} %pad_clamp_fusion), kind=kCustom, calls=%fused_computation | custom fusion | bytes 16778240 | tf_op jit(solution)/shard_map/gather | solution.py:22
  74.2 189.3 %all-gather.5.cloned.1.call-done = bf16[8,32,256,256]{3,2,1,0:T(8,128)(2,1)} async-done(((bf16[8,32,64,256]{3,2,1,0:T(8,128)(2,1)}), bf16[8,32,256,256]{3,2,1,0:T(8,128)(2,1)}) %all-gather.5.cloned.1.call-update) | async-done | bytes 33554448 | tf_op jit(solution)/shard_map/all_gather | solution.py:29
  263.5 15.6 %fusion.3 = bf16[8,32,64,256]{3,2,1,0:T(8,128)(2,1)S(1)} fusion(bf16[8,32,256,256]{3,2,1,0:T(8,128)(2,1)} %all-gather.5.cloned.1.call-done, bf16[8,32,64,256]{3,2,1,0:T(8,128)(2,1)} %bitcast.390, pred[8,32]{1,0:T(8,128)(4,1)S(1)} %compare_and_fusion), kind=kOutput, calls=%fused_computation.4 | convolution fusion | flops 2155872256 | bytes 50331904 | tf_op jit(solution)/shard_map/pqab,pqbc->pqac/dot_general | solution.py:30
  279.1 2.9 fusion.11
  282.0 2.8 fusion.12
  284.8 2.7 fusion.13
  287.6 2.9 fusion.14
  290.5 2.8 fusion.15
  293.3 2.8 fusion.16
  297.9 1.9 fusion.18
  299.7 1.8 fusion.19
  301.6 1.8 fusion.20
  305.2 1.8 fusion.22
  307.0 1.8 fusion.23
  308.8 1.9 fusion.24
  312.5 1.8 fusion.26
  314.3 1.8 fusion.27
  316.1 1.8 fusion.28
  317.9 1.9 fusion.29
  321.6 1.8 fusion.31
  323.4 1.8 fusion.32
  327.0 1.8 fusion.34
  328.8 1.8 fusion.35
  330.6 1.8 fusion.36
  332.4 1.9 fusion.37
  337.9 1.8 fusion.40
  341.5 1.8 fusion.42
  343.3 23.3 %bitcast_add_fusion = f32[8,256,256]{2,1,0:T(8,128)} fusion(f32[8,256,256]{1,2,0:T(8,128)} %fusion.11, f32[8,256,256]{1,2,0:T(8,128)} %fusion.12, f32[8,256,256]{1,2,0:T(8,128)} %fusion.13, f32[8,256,256]{1,2,0:T(8,128)} %fusion.14, f32[8,256,256]{1,2,0:T(8,128)} %fusion.15, f32[8,256,256]{1,2,0:T(8,128)} %fusion.16, f32[8,256,256]{1,2,0:T(8,128)} %fusion.17, ...), kind=kOutput, calls=%fused_computation.6 | convolution fusion | flops 100663296 | bytes 70008832 | tf_op jit(solution)/shard_map/pab,pbc->pac/dot_general | solution.py:26
  366.7 31.3 %reduce-scatter.2.cloned.1.call-done = f32[8,64,256]{2,1,0:T(8,128)} async-done(((f32[8,256,256]{2,1,0:T(8,128)}), f32[8,64,256]{2,1,0:T(8,128)}) %reduce-scatter.2.cloned.1.call-update) | async-done | bytes 524304 | tf_op jit(solution)/shard_map/reduce_scatter | solution.py:41
  398.0 2.1 fusion.9
  (39 shorter events, 17.6 us)
Async XLA Ops:
  6.5 336.8 %copy-start = (bf16[8,256,256]{2,1,0:T(8,128)(2,1)S(1)}, bf16[8,256,256]{2,1,0:T(8,128)(2,1)}, u32[]{:S(2)}) copy-start(bf16[8,256,256]{2,1,0:T(8,128)(2,1)} %param.9) | copy-start | bytes 3145732
  6.5 55.3 %all-gather.3.cloned.1.call-start = ((), (), s32[]{:S(2)}) async-start(), calls=%async_computation.1 | async-start | bytes 2359296 | tf_op jit(solution)/shard_map/all_gather | solution.py:20
  9.9 0.8 copy-start.4
  9.9 0.9 copy-start.2
  9.9 253.6 %all-gather.5.cloned.1.call-start = ((), (), s32[]{:S(2)}) async-start(), calls=%async_computation.2 | async-start | bytes 41943040 | tf_op jit(solution)/shard_map/all_gather | solution.py:29
  10.7 387.3 %reduce-scatter.2.cloned.1.call-start = ((), (), s32[]{:S(2)}) async-start(), calls=%async_computation.3 | async-start | bytes 2621440 | tf_op jit(solution)/shard_map/reduce_scatter | solution.py:41
  279.1 17.0 %slice-start = ((s8[8388608]{0:T(1024)(128)(4,1)}), s8[4194304]{0:T(1024)(128)(4,1)S(1)}, s32[]{:S(2)}) async-start(s8[8388608]{0:T(1024)(128)(4,1)} %bitcast.388), calls=%async_computation.4 | async-start | bytes 8388608
  287.6 8.5 %slice-start.1 = ((s8[8388608]{0:T(1024)(128)(4,1)}), s8[4194304]{0:T(1024)(128)(4,1)S(1)}, s32[]{:S(2)}) async-start(s8[8388608]{0:T(1024)(128)(4,1)} %bitcast.388), calls=%async_computation.5 | async-start | bytes 8388608
  339.7 3.6 copy-start.1
  366.6 31.3 %copy-start.3 = (bf16[8,64,256]{2,1,0:T(8,128)(2,1)S(1)}, bf16[8,64,256]{2,1,0:T(8,128)(2,1)}, u32[]{:S(2)}) copy-start(bf16[8,64,256]{2,1,0:T(8,128)(2,1)} %param.10) | copy-start | bytes 786436
Sparse Core Ops, SparseCore 0:
  10.0 51.7 all-gather.2
  63.4 200.0 all-gather.4
  366.8 31.1 reduce-scatter.1
where the time goes:
time: 407 us
  waiting for transfers between devices  271 us (67%)
  matrix products  105 us (26%)
  local copies, waits for them, and re-layouts  13.4 us (3%)
  between operations  13.2 us (3%)
    all_gather x1, waiting for transfers between devices, shards(): lax.all_gather(intersections, 'cols', axis=2, tiled=True)  189 us
    dot_general x32, matrix products, shards(): jnp.einsum('pcd,pca->pda', intersections[:, slot_index], projected[:, slo...  64.2 us
    all_gather x1, waiting for transfers between devices, shards(): piece = lax.all_gather(masked, 'pairs', axis=0, tiled=True)  50.1 us
    reduce_scatter x1, waiting for transfers between devices, shards(): lax.psum_scatter(partial_value, 'cols', scatter_dimension=1, tiled=True)  31.3 us
    dot_general x1, matrix products, shards(): jnp.einsum('pab,pbc->pac', fock_cols, masked, preferred_element_type=jnp....  23.3 us
    dot_general x1, matrix products, shards(): jnp.einsum('pqab,pqbc->pqac', partner_blocks, whole_intersections, prefer...  15.6 us
    gather x1, local copies, waits for them, and re-layouts, shards(): picked = piece[jnp.clip(linear, 0, piece.shape[0] - 1)]  12.4 us
  transfers between devices with their start and end apart: 3, of which 3 were waited for; matrix products, arithmetic and copies ran while one was open for 3% of the time, Pallas kernels for 0%

commit v1 on v0

--- a/solution.py
+++ b/solution.py
@@ -17,7 +17,14 @@
     masked = jnp.where(keep, amplitudes, jnp.zeros_like(amplitudes))
     linear = partners.reshape(-1)
     empty = jnp.zeros((local_pairs * CPL, share, width), jnp.bfloat16)
-    piece = lax.all_gather(masked, "pairs", axis=0, tiled=True)
+    size = lax.axis_size("pairs")
+    route = [(i, (i + 1) % size) for i in range(size)]
+    parts = [masked]
+    for stride in range(1, size):
+        parts = [lax.ppermute(parts[0], "pairs", route), *parts]
+    whole = jnp.concatenate(parts, axis=0)
+    shift = (lax.axis_index("pairs") + 1) * parts[-1].shape[0]
+    piece = jnp.roll(whole, shift, axis=0)
     present = (linear >= 0) & (linear < piece.shape[0])
     picked = piece[jnp.clip(linear, 0, piece.shape[0] - 1)]
     partner_flat = jnp.where(present[:, None, None], picked, empty)

time: 407 us -> 357 us (0.88)
  waiting for transfers between devices: 271 us -> 222 us
    ppermute x0 -> x7, waiting for transfers between devices: none -> 64.8 us  [shards(): parts = [lax.ppermute(parts[0], 'pairs', route), *parts]]
    all_gather x1, waiting for transfers between devices: 189 us -> 125 us  [shards(): lax.all_gather(intersections, 'cols', axis=2, tiled=True)]
    all_gather x1 -> x0, waiting for transfers between devices: 50.1 us -> none  [shards(): piece = lax.all_gather(masked, 'pairs', axis=0, tiled=True)]
  transfers between devices with their start and end apart: 3 -> 9, of which waited for: 3 -> 9; matrix products, arithmetic and copies ran while one was open for 3% -> 3% of each run, Pallas kernels for 0% -> 0%
where the time goes in v1:
time: 357 us
  waiting for transfers between devices  222 us (62%)
  matrix products  105 us (29%)
  between operations  13.7 us (4%)
  local copies, waits for them, and re-layouts  12 us (3%)
    all_gather x1, waiting for transfers between devices, shards(): lax.all_gather(intersections, 'cols', axis=2, tiled=True)  125 us
    ppermute x7, waiting for transfers between devices, shards(): parts = [lax.ppermute(parts[0], 'pairs', route), *parts]  64.8 us
    dot_general x32, matrix products, shards(): jnp.einsum('pcd,pca->pda', intersections[:, slot_index], projected[:, slo...  64.1 us
    reduce_scatter x1, waiting for transfers between devices, shards(): lax.psum_scatter(partial_value, 'cols', scatter_dimension=1, tiled=True)  31.3 us
    dot_general x1, matrix products, shards(): jnp.einsum('pab,pbc->pac', fock_cols, masked, preferred_element_type=jnp....  23.3 us
    dot_general x1, matrix products, shards(): jnp.einsum('pqab,pqbc->pqac', partner_blocks, whole_intersections, prefer...  15.6 us
    gather x1, local copies, waits for them, and re-layouts, shards(): picked = piece[jnp.clip(linear, 0, piece.shape[0] - 1)]  8.59 us
  transfers between devices with their start and end apart: 9, of which 9 were waited for; matrix products, arithmetic and copies ran while one was open for 3% of the time, Pallas kernels for 0%

profile of v1, /device:TPU:0, one launch (start us, length us, event | category | flops | bytes accessed | tf_op | source)
XLA Modules:
  0.0 356.5 jit_solution(10079852008926161571)
XLA Ops:
  7.7 3.0 collective-permute-start
  10.8 9.3 %collective-permute-done = bf16[8,64,256]{2,1,0:T(8,128)(2,1)S(1)} collective-permute-done((bf16[8,64,256]{2,1,0:T(8,128)(2,1)S(1)}, bf16[8,64,256]{2,1,0:T(8,128)(2,1)S(1)}, u32[]{:S(2)}, u32[]{:S(2)}) %collective-permute-start) | collective-permute-done | bytes 262176 | tf_op jit(solution)/shard_map/ppermute | solution.py:24
  20.1 10.2 %collective-permute-done.1 = bf16[8,64,256]{2,1,0:T(8,128)(2,1)S(1)} collective-permute-done((bf16[8,64,256]{2,1,0:T(8,128)(2,1)S(1)}, bf16[8,64,256]{2,1,0:T(8,128)(2,1)S(1)}, u32[]{:S(2)}, u32[]{:S(2)}) %collective-permute-start.1) | collective-permute-done | bytes 262176 | tf_op jit(solution)/shard_map/ppermute | solution.py:24
  30.3 9.3 %collective-permute-done.2 = bf16[8,64,256]{2,1,0:T(8,128)(2,1)S(1)} collective-permute-done((bf16[8,64,256]{2,1,0:T(8,128)(2,1)S(1)}, bf16[8,64,256]{2,1,0:T(8,128)(2,1)S(1)}, u32[]{:S(2)}, u32[]{:S(2)}) %collective-permute-start.2) | collective-permute-done | bytes 262176 | tf_op jit(solution)/shard_map/ppermute | solution.py:24
  39.6 9.1 %collective-permute-done.3 = bf16[8,64,256]{2,1,0:T(8,128)(2,1)S(1)} collective-permute-done((bf16[8,64,256]{2,1,0:T(8,128)(2,1)S(1)}, bf16[8,64,256]{2,1,0:T(8,128)(2,1)S(1)}, u32[]{:S(2)}, u32[]{:S(2)}) %collective-permute-start.3) | collective-permute-done | bytes 262176 | tf_op jit(solution)/shard_map/ppermute | solution.py:24
  49.2 8.6 %collective-permute-done.4 = bf16[8,64,256]{2,1,0:T(8,128)(2,1)S(1)} collective-permute-done((bf16[8,64,256]{2,1,0:T(8,128)(2,1)S(1)}, bf16[8,64,256]{2,1,0:T(8,128)(2,1)S(1)}, u32[]{:S(2)}, u32[]{:S(2)}) %collective-permute-start.4) | collective-permute-done | bytes 262176 | tf_op jit(solution)/shard_map/ppermute | solution.py:24
  58.2 9.2 %collective-permute-done.5 = bf16[8,64,256]{2,1,0:T(8,128)(2,1)S(1)} collective-permute-done((bf16[8,64,256]{2,1,0:T(8,128)(2,1)S(1)}, bf16[8,64,256]{2,1,0:T(8,128)(2,1)S(1)}, u32[]{:S(2)}, u32[]{:S(2)}) %collective-permute-start.5) | collective-permute-done | bytes 262176 | tf_op jit(solution)/shard_map/ppermute | solution.py:24
  67.5 9.1 %collective-permute-done.6 = bf16[8,64,256]{2,1,0:T(8,128)(2,1)} collective-permute-done((bf16[8,64,256]{2,1,0:T(8,128)(2,1)S(1)}, bf16[8,64,256]{2,1,0:T(8,128)(2,1)}, u32[]{:S(2)}, u32[]{:S(2)}) %collective-permute-start.6) | collective-permute-done | bytes 262176 | tf_op jit(solution)/shard_map/ppermute | solution.py:24
  79.4 8.6 %gather_fusion = bf16[256,64,256]{2,1,0:T(8,128)(2,1)} fusion(bf16[64,64,256]{2,1,0:T(8,128)(2,1)S(1)} %constant_dynamic-slice_fusion, s32[1024]{0:T(1024)S(1)} %pad_clamp_fusion), kind=kCustom, calls=%fused_computation | custom fusion | bytes 16778240 | tf_op jit(solution)/shard_map/gather | solution.py:29
  88.0 125.2 %all-gather.2.cloned.1.call-done = bf16[8,32,256,256]{3,2,1,0:T(8,128)(2,1)} async-done(((bf16[8,32,64,256]{3,2,1,0:T(8,128)(2,1)}), bf16[8,32,256,256]{3,2,1,0:T(8,128)(2,1)}) %all-gather.2.cloned.1.call-update) | async-done | bytes 33554448 | tf_op jit(solution)/shard_map/all_gather | solution.py:36
  213.2 15.6 %fusion.3 = bf16[8,32,64,256]{3,2,1,0:T(8,128)(2,1)S(1)} fusion(bf16[8,32,256,256]{3,2,1,0:T(8,128)(2,1)} %all-gather.2.cloned.1.call-done, bf16[8,32,64,256]{3,2,1,0:T(8,128)(2,1)} %bitcast.390, pred[8,32]{1,0:T(8,128)(4,1)S(1)} %compare_and_fusion), kind=kOutput, calls=%fused_computation.4 | convolution fusion | flops 2155872256 | bytes 50331904 | tf_op jit(solution)/shard_map/pqab,pqbc->pqac/dot_general | solution.py:37
  228.8 2.9 fusion.11
  231.7 2.8 fusion.12
  234.5 2.7 fusion.13
  237.2 2.9 fusion.14
  240.2 2.8 fusion.15
  242.9 2.8 fusion.16
  247.6 1.8 fusion.18
  249.4 1.8 fusion.19
  251.2 1.8 fusion.20
  256.7 1.8 fusion.23
  258.5 1.9 fusion.24
  262.1 1.8 fusion.26
  267.6 1.9 fusion.29
  273.0 1.8 fusion.32
  276.6 1.8 fusion.34
  282.1 1.9 fusion.37
  287.5 1.8 fusion.40
  291.1 1.8 fusion.42
  293.0 23.3 %bitcast_add_fusion = f32[8,256,256]{2,1,0:T(8,128)} fusion(f32[8,256,256]{1,2,0:T(8,128)} %fusion.11, f32[8,256,256]{1,2,0:T(8,128)} %fusion.12, f32[8,256,256]{1,2,0:T(8,128)} %fusion.13, f32[8,256,256]{1,2,0:T(8,128)} %fusion.14, f32[8,256,256]{1,2,0:T(8,128)} %fusion.15, f32[8,256,256]{1,2,0:T(8,128)} %fusion.16, f32[8,256,256]{1,2,0:T(8,128)} %fusion.17, ...), kind=kOutput, calls=%fused_computation.6 | convolution fusion | flops 100663296 | bytes 70008832 | tf_op jit(solution)/shard_map/pab,pbc->pac/dot_general | solution.py:33
  316.3 31.3 %reduce-scatter.2.cloned.1.call-done = f32[8,64,256]{2,1,0:T(8,128)} async-done(((f32[8,256,256]{2,1,0:T(8,128)}), f32[8,64,256]{2,1,0:T(8,128)}) %reduce-scatter.2.cloned.1.call-update) | async-done | bytes 524304 | tf_op jit(solution)/shard_map/reduce_scatter | solution.py:48
  347.6 2.1 fusion.9
  (69 shorter events, 29.8 us)
Async XLA Ops:
  6.5 286.4 %copy-start = (bf16[8,256,256]{2,1,0:T(8,128)(2,1)S(1)}, bf16[8,256,256]{2,1,0:T(8,128)(2,1)}, u32[]{:S(2)}) copy-start(bf16[8,256,256]{2,1,0:T(8,128)(2,1)} %param.9) | copy-start | bytes 3145732
  6.5 0.8 copy-start.5
  6.5 1.1 copy-start.2
  6.5 42.1 %copy-start.1 = (f32[8,32]{1,0:T(8,128)S(1)}, f32[8,32]{1,0:T(8,128)}, u32[]{:S(2)}) copy-start(f32[8,32]{1,0:T(8,128)} %param.13) | copy-start | bytes 3076
  6.5 42.6 %copy-start.4 = (s32[8,32]{1,0:T(8,128)S(1)}, s32[8,32]{1,0:T(8,128)}, u32[]{:S(2)}) copy-start(s32[8,32]{1,0:T(8,128)} %param.12) | copy-start | bytes 3076
  6.5 206.6 %all-gather.2.cloned.1.call-start = ((), (), s32[]{:S(2)}) async-start(), calls=%async_computation.1 | async-start | bytes 41943040 | tf_op jit(solution)/shard_map/all_gather | solution.py:36
  7.3 340.3 %reduce-scatter.2.cloned.1.call-start = ((), (), s32[]{:S(2)}) async-start(), calls=%async_computation.2 | async-start | bytes 2621440 | tf_op jit(solution)/shard_map/reduce_scatter | solution.py:48
  7.7 12.4 %collective-permute-start = (bf16[8,64,256]{2,1,0:T(8,128)(2,1)S(1)}, bf16[8,64,256]{2,1,0:T(8,128)(2,1)S(1)}, u32[]{:S(2)}, u32[]{:S(2)}) collective-permute-start(bf16[8,64,256]{2,1,0:T(8,128)(2,1)S(1)} %and_select_fusion), channel_id=1, source_target_pairs={{0,4},{4,8},{8,12},{12,16},{16,20},{20,24},{24,28},{28,0},{1,5},{5... | collective-permute-start | bytes 786440 | tf_op jit(solution)/shard_map/ppermute | solution.py:24
  20.1 10.2 %collective-permute-start.1 = (bf16[8,64,256]{2,1,0:T(8,128)(2,1)S(1)}, bf16[8,64,256]{2,1,0:T(8,128)(2,1)S(1)}, u32[]{:S(2)}, u32[]{:S(2)}) collective-permute-start(bf16[8,64,256]{2,1,0:T(8,128)(2,1)S(1)} %collective-permute-done), channel_id=1, source_target_pairs={{0,4},{4,8},{8,12},{12,16},{16,20},{20,24},{24,28},{28,0},{1,5},{5... | collective-permute-start | bytes 786440 | tf_op jit(solution)/shard_map/ppermute | solution.py:24
  30.3 9.3 %collective-permute-start.2 = (bf16[8,64,256]{2,1,0:T(8,128)(2,1)S(1)}, bf16[8,64,256]{2,1,0:T(8,128)(2,1)S(1)}, u32[]{:S(2)}, u32[]{:S(2)}) collective-permute-start(bf16[8,64,256]{2,1,0:T(8,128)(2,1)S(1)} %collective-permute-done.1), channel_id=1, source_target_pairs={{0,4},{4,8},{8,12},{12,16},{16,20},{20,24},{24,28},{28,0},{1,5},{5... | collective-permute-start | bytes 786440 | tf_op jit(solution)/shard_map/ppermute | solution.py:24
  39.6 9.1 %collective-permute-start.3 = (bf16[8,64,256]{2,1,0:T(8,128)(2,1)S(1)}, bf16[8,64,256]{2,1,0:T(8,128)(2,1)S(1)}, u32[]{:S(2)}, u32[]{:S(2)}) collective-permute-start(bf16[8,64,256]{2,1,0:T(8,128)(2,1)S(1)} %collective-permute-done.2), channel_id=1, source_target_pairs={{0,4},{4,8},{8,12},{12,16},{16,20},{20,24},{24,28},{28,0},{1,5},{5... | collective-permute-start | bytes 786440 | tf_op jit(solution)/shard_map/ppermute | solution.py:24
  48.7 9.1 %collective-permute-start.4 = (bf16[8,64,256]{2,1,0:T(8,128)(2,1)S(1)}, bf16[8,64,256]{2,1,0:T(8,128)(2,1)S(1)}, u32[]{:S(2)}, u32[]{:S(2)}) collective-permute-start(bf16[8,64,256]{2,1,0:T(8,128)(2,1)S(1)} %collective-permute-done.3), channel_id=1, source_target_pairs={{0,4},{4,8},{8,12},{12,16},{16,20},{20,24},{24,28},{28,0},{1,5},{5... | collective-permute-start | bytes 786440 | tf_op jit(solution)/shard_map/ppermute | solution.py:24
  57.8 9.7 %collective-permute-start.5 = (bf16[8,64,256]{2,1,0:T(8,128)(2,1)S(1)}, bf16[8,64,256]{2,1,0:T(8,128)(2,1)S(1)}, u32[]{:S(2)}, u32[]{:S(2)}) collective-permute-start(bf16[8,64,256]{2,1,0:T(8,128)(2,1)S(1)} %collective-permute-done.4), channel_id=1, source_target_pairs={{0,4},{4,8},{8,12},{12,16},{16,20},{20,24},{24,28},{28,0},{1,5},{5... | collective-permute-start | bytes 786440 | tf_op jit(solution)/shard_map/ppermute | solution.py:24
  67.4 9.2 %collective-permute-start.6 = (bf16[8,64,256]{2,1,0:T(8,128)(2,1)S(1)}, bf16[8,64,256]{2,1,0:T(8,128)(2,1)}, u32[]{:S(2)}, u32[]{:S(2)}) collective-permute-start(bf16[8,64,256]{2,1,0:T(8,128)(2,1)S(1)} %collective-permute-done.5), channel_id=1, source_target_pairs={{0,4},{4,8},{8,12},{12,16},{16,20},{20,24},{24,28},{28,0},{1,5},{5... | collective-permute-start | bytes 786440 | tf_op jit(solution)/shard_map/ppermute | solution.py:24
  228.8 17.0 %slice-start = ((s8[8388608]{0:T(1024)(128)(4,1)}), s8[4194304]{0:T(1024)(128)(4,1)S(1)}, s32[]{:S(2)}) async-start(s8[8388608]{0:T(1024)(128)(4,1)} %bitcast.388), calls=%async_computation.3 | async-start | bytes 8388608
  237.2 8.6 %slice-start.1 = ((s8[8388608]{0:T(1024)(128)(4,1)}), s8[4194304]{0:T(1024)(128)(4,1)S(1)}, s32[]{:S(2)}) async-start(s8[8388608]{0:T(1024)(128)(4,1)} %bitcast.388), calls=%async_computation.4 | async-start | bytes 8388608
  316.2 31.4 %copy-start.3 = (bf16[8,64,256]{2,1,0:T(8,128)(2,1)S(1)}, bf16[8,64,256]{2,1,0:T(8,128)(2,1)}, u32[]{:S(2)}) copy-start(bf16[8,64,256]{2,1,0:T(8,128)(2,1)} %param.10) | copy-start | bytes 786436
Sparse Core Ops, SparseCore 0:
  8.9 204.2 all-gather.1
  316.4 31.1 reduce-scatter.1
